TPU v7x, 512 devices: a whole 4x8x8 slice. The times are simulated.
512 devices in a mesh: vocab: 64 (over y, x, core), grp: 8 (over z).
Axes of the slice: x: 4, y: 8, z: 8, core: 2. Of those that a mesh axis runs over, the one named last changes fastest.
Arguments:
- hidden: bfloat16 [2048, 4096], P('grp'), may hold values from -240 to 240
- head_weight: bfloat16 [4096, 32768], P('grp', 'vocab'), may hold values from -0.25 to 0.25
- cluster_weight: bfloat16 [4096, 3], replicated, may hold values from -0.5 to 0.5
- proj_one: bfloat16 [4096, 1024], P('vocab'), may hold values from -0.09375 to 0.09375
- proj_two: bfloat16 [4096, 256], P('vocab'), may hold values from -0.09375 to 0.09375
- proj_three: bfloat16 [4096, 64], P('vocab'), may hold values from -0.09375 to 0.09375
- tail_one: bfloat16 [1024, 65536], P('grp', 'vocab'), may hold values from -0.5 to 0.5
- tail_two: bfloat16 [256, 65536], P('grp', 'vocab'), may hold values from -1 to 1
- tail_three: bfloat16 [64, 65536], P('grp', 'vocab'), may hold values from -2 to 2
- targets: int32 [2048], P('grp'), may hold values from 0 to 229375, as said below
- flags: int32 [2048, 3], P('grp'), may hold values from 0 to 1, as said below
Outputs:
- target_logprob: float32 [2048], P('grp')
- tail_entropy: float32 [2048, 3], P('grp')
Inputs may be any that keep to these rules, and one draw needn't show every extreme that they name: `targets`: a target at or beyond 32768 lies in tail (t - 32768) // 65536. flags[b, c] is 1 whenever the target of sequence b lies in tail c.
All inputs are finite; a program needn't handle non-finite values.
Results may differ from a plain program's by a relative error of at most 0.0092.
Values may be sent and summed in bfloat16 or wider, within the bound.
No kernel may reach another device: no remote copies, remote signals or barrier semaphores. Data moves between devices by JAX's collectives and lax.ppermute only.
A program may use at most 64 MiB of HBM per device.

v0:
```python
import functools

import jax
import jax.numpy as jnp
from jax import lax
from jax.experimental import pallas as pl
from jax.experimental.pallas import tpu as pltpu
from jax.sharding import Mesh
from jax.sharding import PartitionSpec as P


V_HEAD = 32768
TAIL = 65536
VOCAB = ("vocab_0", "vocab_1", "vocab_2")
CHIPS, CORE = VOCAB[:2], VOCAB[2]


def ring(shard, other, axis):
    n = lax.axis_size(axis)
    even = [(i, i ^ 1) for i in range(n)]
    odd = [(i, ((i + 1) ^ 1) - 1 if 0 < i < n - 1 else n - 1 - i) for i in range(n)]
    side = 1 - 2 * (lax.axis_index(axis) % 2)
    streams = {"a": (shard, shard), "b": (other, other)}
    found, offsets = {"a": [], "b": []}, [0]
    for step in range(1, n // 2):
        for name, (one, two) in streams.items():
            came = lax.ppermute(two, axis, even)
            two = lax.ppermute(one, axis, odd)
            streams[name] = (came, two)
            found[name] += [came, two]
        offsets += [side * step, -side * step]
    first = lax.ppermute(streams["a"][1], axis, even)
    second = lax.ppermute(streams["b"][0], axis, odd)
    offsets.append(n // 2)
    owners = (lax.axis_index(axis) + jnp.stack([jnp.int32(k) for k in offsets])) % n
    return found["a"], found["b"], first, second, owners


def copy_for_each(shard, axis):
    n = lax.psum(1, axis)
    copies = jnp.broadcast_to(shard, (n, *shard.shape))
    return lax.all_to_all(copies, axis, split_axis=0, concat_axis=0, tiled=True)


def dot(a, b):
    return jnp.dot(a, b, preferred_element_type=jnp.float32)


def kernel_call(body, out_shape, flops, scratch=(), mib=16):
    vmem = pl.BlockSpec(memory_space=pltpu.VMEM)
    smem = pl.BlockSpec(memory_space=pltpu.SMEM)

    def call(scalars, *arrays):
        return pl.pallas_call(
            body,
            out_shape=out_shape,
            in_specs=[smem] * (scalars is not None) + [vmem] * len(arrays),
            out_specs=jax.tree.map(lambda _: vmem, out_shape),
            scratch_shapes=list(scratch),
            cost_estimate=pl.CostEstimate(flops=flops, bytes_accessed=1 << 20, transcendentals=0),
            compiler_params=pltpu.CompilerParams(vmem_limit_bytes=mib << 20),
        )(*(() if scalars is None else (scalars,)), *arrays)

    return call


def pack_kernel(places, *refs):
    sources, outs, sems = refs[:-3], refs[-3:-1], refs[-1]
    copies = []
    for k, (source, top, height, left, out, at) in enumerate(places):
        copies.append(
            pltpu.make_async_copy(
                sources[source].at[pl.ds(top, height), pl.ds(left, outs[out].shape[1])],
                outs[out].at[pl.ds(at, height), :],
                sems.at[k],
            )
        )
    for copy in copies:
        copy.start()
    for copy in copies:
        copy.wait()


def packed_rows(tails, head, width, rest):
    places, at = [], 0
    for k, tail in enumerate(tails):
        for left in range(0, tail.shape[1], width):
            places.append((k, 0, tail.shape[0], left, 0, at))
            at += tail.shape[0]
    places.append((len(tails), 0, rest, 0, 0, at))
    places.append((len(tails), rest, head.shape[0] - rest, 0, 1, 0))
    return pl.pallas_call(
        functools.partial(pack_kernel, places),
        out_shape=(
            jax.ShapeDtypeStruct((at + rest, width), head.dtype),
            jax.ShapeDtypeStruct((head.shape[0] - rest, width), head.dtype),
        ),
        in_specs=[pl.BlockSpec(memory_space=pltpu.HBM)] * (len(tails) + 1),
        out_specs=(pl.BlockSpec(memory_space=pltpu.VMEM),) * 2,
        scratch_shapes=[pltpu.SemaphoreType.DMA((len(places),))],
    )(*tails, head)


def project_kernel(weight_ref, hidden_ref, out_ref):
    joined = jnp.concatenate([weight_ref[k] for k in range(weight_ref.shape[0])], axis=1)
    out_ref[...] = lax.dot_general(
        joined, hidden_ref[...], (((1,), (1,)), ((), ())), preferred_element_type=jnp.float32
    ).astype(out_ref.dtype)


def spread(block, owner, count):
    tall = jnp.concatenate([block] * count, axis=0)
    row = lax.broadcasted_iota(jnp.int32, tall.shape, 0)
    return tall, row // block.shape[0] == owner


def part_kernel(h, owner_ref, hidden_ref, *refs):
    *refs, head_ref = refs
    count = h.count - 1
    head = None
    for k in range(count):
        for low, block in ((0, refs[k][h.head_at :, :]), (h.rest, refs[count + k][...])):
            at = pl.multiple_of(owner_ref[k] * h.head + low, 128)
            term = dot(hidden_ref[:, pl.ds(at, block.shape[0])], block)
            head = term if head is None else head + term
    head_ref[...] = head


def lift_kernel(h, owner_ref, turned_ref, *refs):
    shard_refs = refs[: h.count - 1]
    proj_ref, one_ref, two_ref, three_ref, wide_ref = refs[h.count - 1 :]
    proj_ref[...] = turned_ref[...].T
    n, half = h.count, h.half
    last = owner_ref[n - 1]
    blank = jnp.zeros((h.one, half), wide_ref.dtype)
    small = jnp.zeros((h.two, half), wide_ref.dtype)
    for side in range(2):
        wide_ref[side, pl.ds(pl.multiple_of(last * h.one, h.one), h.one), :] = blank
        two_ref[side, pl.ds(pl.multiple_of(last * h.two, h.two), h.two), :] = small
    threes = [jnp.zeros((h.three * n, half), jnp.float32)] * 2
    for k, ref in enumerate(shard_refs):
        owner = owner_ref[k]
        for side in range(2):
            wide_ref[side, pl.ds(pl.multiple_of(owner * h.one, h.one), h.one), :] = ref[
                side * h.one : (side + 1) * h.one, :
            ]
            at = 2 * h.one + side * h.two
            two_ref[side, pl.ds(pl.multiple_of(owner * h.two, h.two), h.two), :] = ref[
                at : at + h.two, :
            ]
        both = ref[h.three_at : h.head_at, :].astype(jnp.float32)
        for side in range(2):
            tall, there = spread(both[side * h.three : (side + 1) * h.three], owner, n)
            threes[side] = jnp.where(there, tall, threes[side])
    for side in range(2):
        three_ref[side] = threes[side].astype(three_ref.dtype)
        one_ref[:, side * half : (side + 1) * half] = dot(
            proj_ref[:, : h.one * n], wide_ref[side]
        )


def columns_of(sides, ids, with_mass):
    top = functools.reduce(
        jnp.maximum, [jnp.max(logits, axis=1, keepdims=True) for logits in sides]
    )
    total = mass = pick = jnp.zeros_like(top)
    for side, logits in enumerate(sides):
        expo = jnp.exp(logits - top)
        total = total + jnp.sum(expo, axis=1, keepdims=True)
        if with_mass:
            mass = mass + jnp.sum(expo * logits, axis=1, keepdims=True)
        word = lax.broadcasted_iota(jnp.int32, logits.shape, 1) + side * logits.shape[1]
        pick = pick + jnp.sum(jnp.where(word == ids, logits, 0.0), axis=1, keepdims=True)
    return top, total, mass, pick


def tails_kernel(
    h,
    owner_ref,
    first_ref,
    hidden_ref,
    proj_ref,
    head_ref,
    one_ref,
    two_ref,
    three_ref,
    ids_ref,
    table_ref,
    more_ref,
    wide_ref,
):
    n, half = h.count, h.half
    owner = owner_ref[n - 1]
    rows = hidden_ref.shape[0]
    at = pl.multiple_of(owner * h.head, h.head)
    more_ref[...] = head_ref[...] + dot(
        hidden_ref[:, pl.ds(at, h.rest)], first_ref[h.head_at :, :]
    )
    one_features = proj_ref[:, pl.ds(pl.multiple_of(owner * h.one, h.one), h.one)]
    two_features = proj_ref[:, h.one * n : (h.one + h.two) * n]
    three_features = proj_ref[:, (h.one + h.two) * n : (h.one + h.two + h.three) * n]
    wide_ref[...] = two_ref[...]
    both = first_ref[h.three_at : h.head_at, :].astype(jnp.float32)
    ones, twos, threes = [], [], []
    for side in range(2):
        ones.append(
            one_ref[:, side * half : (side + 1) * half]
            + dot(one_features, first_ref[side * h.one : (side + 1) * h.one, :])
        )
        at = 2 * h.one + side * h.two
        wide_ref[side, pl.ds(pl.multiple_of(owner * h.two, h.two), h.two), :] = first_ref[
            at : at + h.two, :
        ]
        twos.append(dot(two_features, wide_ref[side]))
        tall, there = spread(both[side * h.three : (side + 1) * h.three], owner, n)
        block = jnp.where(there, tall, three_ref[side].astype(jnp.float32))
        threes.append(dot(three_features, block.astype(three_ref.dtype)))
    lane = lax.broadcasted_iota(jnp.int32, (rows, 128), 1)
    table = jnp.zeros((rows, 128), jnp.float32)
    picked = jnp.zeros((rows, 1), jnp.float32)
    for k, sides in enumerate((ones, twos, threes)):
        top, total, mass, pick = columns_of(sides, ids_ref[:, 1 + k : 2 + k], True)
        for place, column in ((1 + k, top), (5 + k, total), (8 + k, mass)):
            table = jnp.where(lane == place, column, table)
        picked = picked + pick
    table_ref[...] = jnp.where(lane == 11, picked, table)


def last_kernel(h, owner_ref, second_ref, hidden_ref, head_ref, table_ref, ids_ref, out_ref):
    at = pl.multiple_of(owner_ref[h.count - 1] * h.head + h.rest, 128)
    head = head_ref[...] + dot(
        hidden_ref[:, pl.ds(at, h.head - h.rest)], second_ref[...]
    )
    top, total, _, pick = columns_of([head], ids_ref[:, 0:1], False)
    table = table_ref[...]
    lane = lax.broadcasted_iota(jnp.int32, table.shape, 1)
    table = jnp.where(lane == 0, top, jnp.where(lane == 4, total, table))
    write_copies((table + jnp.where(lane == 11, pick, 0.0)).T, out_ref)


def write_copies(table, out_ref):
    width = out_ref.shape[2] // 12
    for k in range(12):
        out_ref[:, 0, k * width : (k + 1) * width] = jnp.broadcast_to(
            table[k : k + 1], (out_ref.shape[0], width)
        )


def combined(ref):
    width = ref.shape[2] // 12
    rows = [ref[:, 0, k * width : (k + 1) * width] for k in range(12)]

    def down(combine, array):
        return combine(array, axis=0, keepdims=True)

    tops = [down(jnp.max, row) for row in rows[0:4]]
    scales = [jnp.exp(row - top) for row, top in zip(rows[0:4], tops)]
    sums = [down(jnp.sum, row * scale) for row, scale in zip(rows[4:8], scales)]
    masses = [down(jnp.sum, row * scale) for row, scale in zip(rows[8:11], scales[1:])]
    return [*tops, *sums, *masses, down(jnp.sum, rows[11])]


def merge_kernel(stats_ref, out_ref):
    write_copies(jnp.concatenate(combined(stats_ref), axis=0), out_ref)


def finish_kernel(stats_ref, scores_ref, flags_ref, targets_ref, prob_ref, entropy_ref):
    rows = combined(stats_ref)
    scores, flags, targets = scores_ref[...], flags_ref[...], targets_ref[...]
    top = jnp.maximum(rows[0], jnp.max(scores, axis=0, keepdims=True))
    total = rows[4] * jnp.exp(rows[0] - top) + jnp.sum(
        jnp.exp(scores - top), axis=0, keepdims=True
    )
    head_lse = top + jnp.log(total)
    picked = rows[11]
    for k in range(3):
        lse = rows[1 + k] + jnp.log(rows[5 + k])
        mean = rows[8 + k] / rows[5 + k]
        entropy_ref[k : k + 1, :] = flags[k : k + 1].astype(jnp.float32) * (lse - mean)
        low = V_HEAD + k * TAIL
        inside = jnp.logical_and(targets >= low, targets < low + TAIL)
        picked = picked + jnp.where(inside, scores[k : k + 1] - lse, 0.0)
    prob_ref[...] = picked - head_lse


class Heights:
    def __init__(self, count, one, two, three, head, half):
        self.count, self.one, self.two, self.three = count, one, two, three
        self.head, self.half = head, half
        self.three_at = 2 * (one + two)
        self.head_at = 2 * (one + two + three)
        self.rest = 128


def one_device(
    hidden,
    head_weight,
    cluster_weight,
    proj_one,
    proj_two,
    proj_three,
    tail_one,
    tail_two,
    tail_three,
    targets,
    flags,
):
    rows = hidden.shape[0]
    head_cols = head_weight.shape[1]
    tail_cols = tail_one.shape[1]
    half = tail_cols // 2
    n_chips = lax.psum(1, CHIPS)
    n_grp = lax.axis_size("grp")
    core = lax.axis_index(CORE)
    vocab_index = lax.axis_index(VOCAB)

    tails = (tail_one, tail_two, tail_three)
    h = Heights(n_grp, *(t.shape[0] for t in tails), head_weight.shape[0], half)
    shard, other = packed_rows(tails, head_weight, half, h.rest)
    found, others, first, second, owners = ring(shard, other, "grp")

    widths = (proj_one.shape[1], proj_two.shape[1], proj_three.shape[1])
    total = sum(widths)
    share = -(-total // (2 * n_chips) // 8) * 8
    joined = lax.all_gather(
        jnp.concatenate((proj_one, proj_two, proj_three), axis=1), CORE, axis=0, tiled=True
    )
    turned = jnp.pad(joined.T, ((0, 2 * n_chips * share - total), (0, 0)))
    turned = turned.reshape(2, n_chips, share, joined.shape[0])
    pieces = lax.dynamic_index_in_dim(turned, core, 0, keepdims=False)
    pieces = lax.all_to_all(pieces, CHIPS, split_axis=0, concat_axis=0, tiled=True)
    mine = kernel_call(
        project_kernel,
        jax.ShapeDtypeStruct((share, rows), jnp.bfloat16),
        2 * share * hidden.size,
    )(None, pieces, hidden)
    turned = copy_for_each(mine, CHIPS)
    turned = lax.all_gather(turned, CORE)
    turned = turned.reshape(2 * n_chips * share, rows)

    wide = jnp.bfloat16
    part_call = kernel_call(
        functools.partial(part_kernel, h),
        jax.ShapeDtypeStruct((rows, head_cols), jnp.float32),
        2 * rows * head_weight.size * n_grp,
    )
    head_part = part_call(owners, hidden, shard, *found, other, *others)
    lift_call = kernel_call(
        functools.partial(lift_kernel, h),
        (
            jax.ShapeDtypeStruct((rows, turned.shape[0]), wide),
            jax.ShapeDtypeStruct((rows, tail_cols), jnp.float32),
            jax.ShapeDtypeStruct((2, h.two * n_grp, half), wide),
            jax.ShapeDtypeStruct((2, h.three * n_grp, half), wide),
        ),
        2 * rows * tail_one.size * n_grp,
        [pltpu.VMEM((2, h.one * n_grp, half), wide)],
    )
    proj, one_part, *small_rows = lift_call(owners, turned, shard, *found)

    cluster_logits = dot(hidden, cluster_weight)
    relative = targets - V_HEAD
    cluster = relative // TAIL
    word = relative - cluster * TAIL
    ids = jnp.stack(
        [targets - vocab_index * head_cols]
        + [jnp.where(cluster == k, word - vocab_index * tail_cols, -1) for k in range(3)],
        axis=1,
    )
    near = VOCAB[1:]
    n_near = lax.psum(1, near)
    n_far = lax.axis_size(VOCAB[0])
    tails_call = kernel_call(
        functools.partial(tails_kernel, h),
        (
            jax.ShapeDtypeStruct((rows, 128), jnp.float32),
            jax.ShapeDtypeStruct((rows, head_cols), jnp.float32),
        ),
        2 * rows * shard.size,
        [pltpu.VMEM((2, h.two * n_grp, half), wide)],
    )
    table, head_part = tails_call(
        owners, first, hidden, proj, head_part, one_part, *small_rows, ids
    )
    stats = kernel_call(
        functools.partial(last_kernel, h),
        jax.ShapeDtypeStruct((n_near, 1, 12 * rows), jnp.float32),
        2 * rows * other.size,
        mib=8,
    )(owners, second, hidden, head_part, table, ids)
    stats = lax.all_to_all(stats, near, split_axis=0, concat_axis=0, tiled=True)
    stats = kernel_call(
        merge_kernel, jax.ShapeDtypeStruct((n_far, 1, 12 * rows), jnp.float32), 1 << 20, mib=4
    )(None, stats)
    stats = lax.all_to_all(stats, VOCAB[0], split_axis=0, concat_axis=0, tiled=True)
    target_logprob, entropy = kernel_call(
        finish_kernel,
        (
            jax.ShapeDtypeStruct((1, rows), jnp.float32),
            jax.ShapeDtypeStruct((3, rows), jnp.float32),
        ),
        1 << 20,
        mib=4,
    )(None, stats, cluster_logits.T, flags.T, targets[None])
    return (target_logprob[0], entropy.T)


def solution(mesh):
    finer = Mesh(
        mesh.devices.reshape(8, 4, 2, mesh.shape["grp"]), ("vocab_0", "vocab_1", "vocab_2", "grp")
    )
    in_specs = (
        P("grp", None),
        P("grp", VOCAB),
        P(),
        P(VOCAB, None),
        P(VOCAB, None),
        P(VOCAB, None),
        P("grp", VOCAB),
        P("grp", VOCAB),
        P("grp", VOCAB),
        P("grp"),
        P("grp", None),
    )
    out_specs = (P("grp"), P("grp", None))
    return jax.shard_map(
        one_device, mesh=finer, in_specs=in_specs, out_specs=out_specs, check_vma=False
    )
```

profile of v0, /device:TPU:1, one launch (start us, length us, event | category | flops | bytes accessed | tf_op | source)
XLA Modules:
  0.0 135.6 jit_solution(8761048253413687812)
XLA Ops:
  0.6 0.0 copy-start
  0.7 2.4 %shard_map.122 = (bf16[464,512]{1,0:T(8,128)(2,1)}, bf16[384,512]{1,0:T(8,128)(2,1)}) custom-call(bf16[128,1024]{1,0:T(8,128)(2,1)} %refs_0_.1, bf16[32,1024]{1,0:T(8,128)(2,1)} %refs_1_.1, bf16[8,1024]{1,0:T(8,128)(2,1)} %refs_2_.1, bf16[512,512]{1,0:T(8,128)(2,1)} %refs_3_.1), custom_call_target="tpu_custom_call" | custom-call | tf_op jit(solution)/shard_map/pallas_call | solution.py:92
  3.0 11.5 %collective-permute-start.4 = (bf16[464,512]{1,0:T(8,128)(2,1)}, bf16[464,512]{1,0:T(8,128)(2,1)S(1)}, u32[]{:S(2)}, u32[]{:S(2)}) collective-permute-start(bf16[464,512]{1,0:T(8,128)(2,1)} %get-tuple-element.13.refs_0_), channel_id=1, source_target_pairs={{0,7},{1,2},{2,1},{3,4},{4,3},{5,6},{6,5},{7,0},{8,15},{9,10},{10,... | collective-permute-start | bytes 1425416 | tf_op jit(solution)/shard_map/ppermute | solution.py:28
  14.5 1.9 %collective-permute-start.8 = (bf16[464,512]{1,0:T(8,128)(2,1)}, bf16[464,512]{1,0:T(8,128)(2,1)S(1)}, u32[]{:S(2)}, u32[]{:S(2)}) collective-permute-start(bf16[464,512]{1,0:T(8,128)(2,1)} %get-tuple-element.13.refs_0_), channel_id=1, source_target_pairs={{0,1},{1,0},{2,3},{3,2},{4,5},{5,4},{6,7},{7,6},{8,9},{9,8},{10,11... | collective-permute-start | bytes 1425416 | tf_op jit(solution)/shard_map/ppermute | solution.py:27
  16.5 3.4 %collective-permute-start = (bf16[384,512]{1,0:T(8,128)(2,1)}, bf16[384,512]{1,0:T(8,128)(2,1)}, u32[]{:S(2)}, u32[]{:S(2)}) collective-permute-start(bf16[384,512]{1,0:T(8,128)(2,1)} %get-tuple-element.12.refs_7_), channel_id=1, source_target_pairs={{0,1},{1,0},{2,3},{3,2},{4,5},{5,4},{6,7},{7,6},{8,9},{9,8},{10,11... | collective-permute-start | bytes 1179656 | tf_op jit(solution)/shard_map/ppermute | solution.py:27
  19.8 1.9 %collective-permute-start.11 = (bf16[384,512]{1,0:T(8,128)(2,1)}, bf16[384,512]{1,0:T(8,128)(2,1)}, u32[]{:S(2)}, u32[]{:S(2)}) collective-permute-start(bf16[384,512]{1,0:T(8,128)(2,1)} %get-tuple-element.12.refs_7_), channel_id=1, source_target_pairs={{0,7},{1,2},{2,1},{3,4},{4,3},{5,6},{6,5},{7,0},{8,15},{9,10},{10,... | collective-permute-start | bytes 1179656 | tf_op jit(solution)/shard_map/ppermute | solution.py:28
  21.8 1.0 pad_maximum_fusion
  22.7 3.2 %all_gather.9 = bf16[128,1344]{1,0:T(8,128)(2,1)S(1)} all-gather(bf16[64,1344]{1,0:T(8,128)(2,1)S(1)} %pad_maximum_fusion), channel_id=1, replica_groups=mesh['vocab_0'=8,'vocab_1'=4,'vocab_2'=2,'grp'=8] {'vocab_2'}, dimensions={0}, use_global_device_ids=true | all-gather | bytes 516096 | tf_op jit(solution)/shard_map/all_gather | solution.py:325
  25.9 0.9 copy.21
  26.9 1.0 pad.4
  27.9 0.0 collective-permute-done.4.refs_2_
  27.9 1.9 %collective-permute-start.5 = (bf16[464,512]{1,0:T(8,128)(2,1)S(1)}, bf16[464,512]{1,0:T(8,128)(2,1)}, u32[]{:S(2)}, u32[]{:S(2)}) collective-permute-start(bf16[464,512]{1,0:T(8,128)(2,1)S(1)} %collective-permute-done.4.refs_2_), channel_id=1, source_target_pairs={{0,1},{1,0},{2,3},{3,2},{4,5},{5,4},{6,7},{7,6},{8,9},{9,8},{10,11... | collective-permute-start | bytes 1425416 | tf_op jit(solution)/shard_map/ppermute | solution.py:27
  29.8 0.7 dynamic-slice_bitcast_fusion
  30.5 9.8 %all-to-all-start = ((bf16[32,24,128]{2,1,0:T(8,128)(2,1)}), bf16[32,24,128]{2,1,0:T(8,128)(2,1)}, u32[]{:S(2)}, u32[]{:S(2)}) async-start(bf16[32,24,128]{2,1,0:T(8,128)(2,1)} %dynamic-slice_bitcast_fusion), calls=%async_computation | async-start | bytes 393216 | tf_op jit(solution)/shard_map/all_to_all | solution.py:331
  40.3 0.0 collective-permute-done.refs_8_
  40.3 4.9 %collective-permute-start.1 = (bf16[384,512]{1,0:T(8,128)(2,1)}, bf16[384,512]{1,0:T(8,128)(2,1)}, u32[]{:S(2)}, u32[]{:S(2)}) collective-permute-start(bf16[384,512]{1,0:T(8,128)(2,1)} %collective-permute-done.refs_8_), channel_id=1, source_target_pairs={{0,7},{1,2},{2,1},{3,4},{4,3},{5,6},{6,5},{7,0},{8,15},{9,10},{10,... | collective-permute-start | bytes 1179656 | tf_op jit(solution)/shard_map/ppermute | solution.py:28
  45.2 0.0 collective-permute-done.8.refs_1_
  45.2 1.9 %collective-permute-start.9 = (bf16[464,512]{1,0:T(8,128)(2,1)S(1)}, bf16[464,512]{1,0:T(8,128)(2,1)}, u32[]{:S(2)}, u32[]{:S(2)}) collective-permute-start(bf16[464,512]{1,0:T(8,128)(2,1)S(1)} %collective-permute-done.8.refs_1_), channel_id=1, source_target_pairs={{0,7},{1,2},{2,1},{3,4},{4,3},{5,6},{6,5},{7,0},{8,15},{9,10},{10,... | collective-permute-start | bytes 1425416 | tf_op jit(solution)/shard_map/ppermute | solution.py:28
  47.1 0.0 collective-permute-done.5.refs_3_
  47.1 4.6 %collective-permute-start.6 = (bf16[464,512]{1,0:T(8,128)(2,1)}, bf16[464,512]{1,0:T(8,128)(2,1)}, u32[]{:S(2)}, u32[]{:S(2)}) collective-permute-start(bf16[464,512]{1,0:T(8,128)(2,1)} %collective-permute-done.5.refs_3_), channel_id=1, source_target_pairs={{0,7},{1,2},{2,1},{3,4},{4,3},{5,6},{6,5},{7,0},{8,15},{9,10},{10,... | collective-permute-start | bytes 1425416 | tf_op jit(solution)/shard_map/ppermute | solution.py:28
  51.7 0.7 stack.42
  52.4 0.0 all-to-all-done.weight_ref
  52.4 1.7 %shard_map.123 = bf16[24,256]{1,0:T(8,128)(2,1)S(1)} custom-call(bf16[32,24,128]{2,1,0:T(8,128)(2,1)} %all-to-all-done.weight_ref, bf16[256,4096]{1,0:T(8,128)(2,1)S(1)} %copy-done.1), custom_call_target="tpu_custom_call" | custom-call | flops 50331648 | bytes 1048576 | tf_op jit(solution)/shard_map/pallas_call | solution.py:54
  54.1 0.8 broadcast_in_dim.10
  54.9 9.3 %all-to-all-start.1 = ((bf16[32,24,256]{2,1,0:T(8,128)(2,1)}), bf16[32,24,256]{2,1,0:T(8,128)(2,1)}, u32[]{:S(2)}, u32[]{:S(2)}) async-start(bf16[32,24,256]{2,1,0:T(8,128)(2,1)} %broadcast_in_dim.10), calls=%async_computation.1 | async-start | bytes 786432 | tf_op jit(solution)/shard_map/all_to_all | solution.py:42
  64.2 0.0 collective-permute-done.11.refs_9_
  64.2 1.9 %collective-permute-start.12 = (bf16[384,512]{1,0:T(8,128)(2,1)}, bf16[384,512]{1,0:T(8,128)(2,1)}, u32[]{:S(2)}, u32[]{:S(2)}) collective-permute-start(bf16[384,512]{1,0:T(8,128)(2,1)} %collective-permute-done.11.refs_9_), channel_id=1, source_target_pairs={{0,1},{1,0},{2,3},{3,2},{4,5},{5,4},{6,7},{7,6},{8,9},{9,8},{10,11... | collective-permute-start | bytes 1179656 | tf_op jit(solution)/shard_map/ppermute | solution.py:27
  66.2 0.7 compare_select_fusion.4
  66.8 0.0 collective-permute-done.1.refs_11_
  66.9 3.4 %collective-permute-start.2 = (bf16[384,512]{1,0:T(8,128)(2,1)}, bf16[384,512]{1,0:T(8,128)(2,1)}, u32[]{:S(2)}, u32[]{:S(2)}) collective-permute-start(bf16[384,512]{1,0:T(8,128)(2,1)} %collective-permute-done.1.refs_11_), channel_id=1, source_target_pairs={{0,1},{1,0},{2,3},{3,2},{4,5},{5,4},{6,7},{7,6},{8,9},{9,8},{10,11... | collective-permute-start | bytes 1179656 | tf_op jit(solution)/shard_map/ppermute | solution.py:27
  70.2 0.7 compare_select_fusion.3
  70.9 4.1 %collective-permute-done.12.refs_10_ = bf16[384,512]{1,0:T(8,128)(2,1)} collective-permute-done((bf16[384,512]{1,0:T(8,128)(2,1)}, bf16[384,512]{1,0:T(8,128)(2,1)}, u32[]{:S(2)}, u32[]{:S(2)}) %collective-permute-start.12) | collective-permute-done | bytes 393248 | tf_op jit(solution)/shard_map/ppermute | solution.py:27
  75.0 1.9 %collective-permute-start.13 = (bf16[384,512]{1,0:T(8,128)(2,1)}, bf16[384,512]{1,0:T(8,128)(2,1)}, u32[]{:S(2)}, u32[]{:S(2)}) collective-permute-start(bf16[384,512]{1,0:T(8,128)(2,1)} %collective-permute-done.12.refs_10_), channel_id=1, source_target_pairs={{0,7},{1,2},{2,1},{3,4},{4,3},{5,6},{6,5},{7,0},{8,15},{9,10},{10,... | collective-permute-start | bytes 1179656 | tf_op jit(solution)/shard_map/ppermute | solution.py:28
  77.0 0.0 collective-permute-done.9.refs_4_
  77.0 2.2 %collective-permute-start.10 = (bf16[464,512]{1,0:T(8,128)(2,1)}, bf16[464,512]{1,0:T(8,128)(2,1)}, u32[]{:S(2)}, u32[]{:S(2)}) collective-permute-start(bf16[464,512]{1,0:T(8,128)(2,1)} %collective-permute-done.9.refs_4_), channel_id=1, source_target_pairs={{0,1},{1,0},{2,3},{3,2},{4,5},{5,4},{6,7},{7,6},{8,9},{9,8},{10,11... | collective-permute-start | bytes 1425416 | tf_op jit(solution)/shard_map/ppermute | solution.py:27
  79.2 0.0 collective-permute-done.6.refs_6_
  79.2 3.1 %collective-permute-start.7 = (bf16[464,512]{1,0:T(8,128)(2,1)}, bf16[464,512]{1,0:T(8,128)(2,1)}, u32[]{:S(2)}, u32[]{:S(2)}) collective-permute-start(bf16[464,512]{1,0:T(8,128)(2,1)} %collective-permute-done.6.refs_6_), channel_id=1, source_target_pairs={{0,1},{1,0},{2,3},{3,2},{4,5},{5,4},{6,7},{7,6},{8,9},{9,8},{10,11... | collective-permute-start | bytes 1425416 | tf_op jit(solution)/shard_map/ppermute | solution.py:32
  82.3 1.2 and_select_fusion.1.owner_ref
  83.5 0.0 collective-permute-done.2.refs_12_
  83.5 4.6 %collective-permute-start.3 = (bf16[384,512]{1,0:T(8,128)(2,1)}, bf16[384,512]{1,0:T(8,128)(2,1)}, u32[]{:S(2)}, u32[]{:S(2)}) collective-permute-start(bf16[384,512]{1,0:T(8,128)(2,1)} %collective-permute-done.2.refs_12_), channel_id=1, source_target_pairs={{0,7},{1,2},{2,1},{3,4},{4,3},{5,6},{6,5},{7,0},{8,15},{9,10},{10,... | collective-permute-start | bytes 1179656 | tf_op jit(solution)/shard_map/ppermute | solution.py:33
  88.1 0.6 pad_add_fusion
  88.7 1.5 %copy.22.ids_ref = s32[256,4]{1,0:T(8,128)} copy(s32[256,4]{0,1:T(4,128)} %pad_add_fusion) | data formatting | bytes 8192 | tf_op jit(solution)/shard_map/stack | solution.py:365
  90.2 0.0 all-to-all-done.1
  90.2 8.9 %all-gather = bf16[64,24,256]{2,1,0:T(8,128)(2,1)S(1)} all-gather(bf16[32,24,256]{2,1,0:T(8,128)(2,1)} %all-to-all-done.1), channel_id=2, replica_groups=mesh['vocab_0'=8,'vocab_1'=4,'vocab_2'=2,'grp'=8] {'vocab_2'}, dimensions={0}, use_global_device_ids=true | all-gather | bytes 1179648 | tf_op jit(solution)/shard_map/all_gather | solution.py:338
  99.0 0.0 collective-permute-done.10.refs_5_
  99.0 0.0 copy-done.2
  99.1 0.0 copy-start.6
  99.1 0.7 copy-done.6
  99.8 2.4 %shard_map.124 = (bf16[256,1536]{1,0:T(8,128)(2,1)S(1)}, f32[256,1024]{1,0:T(8,128)S(1)}, bf16[2,256,512]{2,1,0:T(8,128)(2,1)S(1)}, bf16[2,64,512]{2,1,0:T(8,128)(2,1)S(1)}) custom-call(s32[8]{0:T(128)S(1)} %copy-done.6, bf16[1536,256]{1,0:T(8,128)(2,1)S(1)} %bitcast.21, bf16[464,512]{1,0:T(8,128)(2,1)S(1)} %copy-done.2, ...), custom_call_target="tpu_custom_call" | custom-call | flops 536870912 | bytes 1048576 | tf_op jit(solution)/shard_map/pallas_call | solution.py:54
  102.2 0.0 copy-start.3
  102.2 0.0 collective-permute-done.13.refs_13_
  102.2 3.8 %shard_map.125.head_ref = f32[256,512]{1,0:T(8,128)S(1)} custom-call(s32[8]{0:T(128)S(1)} %copy-done.7, bf16[256,4096]{1,0:T(8,128)(2,1)S(1)} %copy-done.1, bf16[464,512]{1,0:T(8,128)(2,1)S(1)} %copy-done.2, bf16[464,512]{1,0:T(8,128)(2,1)S(1)} %collective-permute-done.8.refs_1_, bf16[464,512]{1,0:T(8,128)(2,1)S(1)} %collective-permute-done.4.refs_2_, ...), custom_call_target="tpu_custom_call" | custom-call | flops 1073741824 | bytes 1048576 | tf_op jit(solution)/shard_map/pallas_call | solution.py:54
  106.0 0.0 collective-permute-done.7.first_ref
  106.0 2.8 %shard_map.126 = (f32[256,128]{1,0:T(8,128)S(1)}, f32[256,512]{1,0:T(8,128)S(1)}) custom-call(s32[8]{0:T(128)S(1)} %copy-done.7, bf16[464,512]{1,0:T(8,128)(2,1)} %collective-permute-done.7.first_ref, bf16[256,4096]{1,0:T(8,128)(2,1)S(1)} %copy-done.1, bf16[256,1536]{1,0:T(8,128)(2,1)S(1)} %get-tuple-element.14.proj_ref, ...), custom_call_target="tpu_custom_call" | custom-call | flops 121634816 | bytes 1048576 | tf_op jit(solution)/shard_map/pallas_call | solution.py:54
  108.8 0.0 collective-permute-done.3.second_ref
  108.8 1.6 %shard_map.127 = f32[8,1,3072]{2,1,0:T(1,128)S(1)} custom-call(s32[8]{0:T(128)S(1)} %copy-done.7, bf16[384,512]{1,0:T(8,128)(2,1)} %collective-permute-done.3.second_ref, bf16[256,4096]{1,0:T(8,128)(2,1)S(1)} %copy-done.1, f32[256,512]{1,0:T(8,128)S(1)} %get-tuple-element.18.head_ref, f32[256,128]{1,0:T(8,128)S(1)} %get-tuple-element.19.table_ref, ...), custom_call_target="tpu_custom_call" | custom-call | flops 100663296 | bytes 1048576 | tf_op jit(solution)/shard_map/pallas_call | solution.py:54
  110.4 0.0 copy-start.5
  110.4 0.0 copy-start.8
  110.4 9.7 %all_to_all.20.stats_ref = f32[8,1,3072]{2,1,0:T(1,128)S(1)} all-to-all(f32[8,1,3072]{2,1,0:T(1,128)S(1)} %shard_map.127), channel_id=1, replica_groups=mesh['vocab_0'=8,'vocab_1'=4,'vocab_2'=2,'grp'=8] {'vocab_1','vocab_2'}, dimensions={0} | all-to-all | bytes 196608 | tf_op jit(solution)/shard_map/all_to_all | solution.py:391
  120.1 0.7 shard_map.128
  120.9 6.4 %all-to-all-start.3 = ((f32[8,1,3072]{2,1,0:T(1,128)}), f32[8,1,3072]{2,1,0:T(1,128)S(1)}, u32[]{:S(2)}, u32[]{:S(2)}) async-start(f32[8,1,3072]{2,1,0:T(1,128)} %shard_map.128), calls=%async_computation.3 | async-start | bytes 196608 | tf_op jit(solution)/shard_map/all_to_all | solution.py:395
  127.2 0.6 fusion.1.scores_ref
  127.9 7.0 %all-to-all-done.3.stats_ref = f32[8,1,3072]{2,1,0:T(1,128)S(1)} async-done(((f32[8,1,3072]{2,1,0:T(1,128)}), f32[8,1,3072]{2,1,0:T(1,128)S(1)}, u32[]{:S(2)}, u32[]{:S(2)}) %all-to-all-start.3) | async-done | bytes 98336 | tf_op jit(solution)/shard_map/all_to_all | solution.py:395
  134.9 0.7 shard_map.129
  (11 shorter events, 0.0 us)
Async XLA Ops:
  0.6 126.6 %copy-start = (bf16[4096,3]{0,1:T(4,128)(2,1)S(1)}, bf16[4096,3]{0,1:T(4,128)(2,1)}, u32[]{:S(2)}) copy-start(bf16[4096,3]{0,1:T(4,128)(2,1)} %param.13) | copy-start | bytes 73732
  0.6 51.8 %copy-start.1 = (bf16[256,4096]{1,0:T(8,128)(2,1)S(1)}, bf16[256,4096]{1,0:T(8,128)(2,1)}, u32[]{:S(2)}) copy-start(bf16[256,4096]{1,0:T(8,128)(2,1)} %hidden_ref.7) | copy-start | bytes 6291460
  3.0 24.8 %collective-permute-start.4 = (bf16[464,512]{1,0:T(8,128)(2,1)}, bf16[464,512]{1,0:T(8,128)(2,1)S(1)}, u32[]{:S(2)}, u32[]{:S(2)}) collective-permute-start(bf16[464,512]{1,0:T(8,128)(2,1)} %get-tuple-element.13.refs_0_), channel_id=1, source_target_pairs={{0,7},{1,2},{2,1},{3,4},{4,3},{5,6},{6,5},{7,0},{8,15},{9,10},{10,... | collective-permute-start | bytes 1425416 | tf_op jit(solution)/shard_map/ppermute | solution.py:28
  14.5 30.7 %collective-permute-start.8 = (bf16[464,512]{1,0:T(8,128)(2,1)}, bf16[464,512]{1,0:T(8,128)(2,1)S(1)}, u32[]{:S(2)}, u32[]{:S(2)}) collective-permute-start(bf16[464,512]{1,0:T(8,128)(2,1)} %get-tuple-element.13.refs_0_), channel_id=1, source_target_pairs={{0,1},{1,0},{2,3},{3,2},{4,5},{5,4},{6,7},{7,6},{8,9},{9,8},{10,11... | collective-permute-start | bytes 1425416 | tf_op jit(solution)/shard_map/ppermute | solution.py:27
  16.5 23.9 %collective-permute-start = (bf16[384,512]{1,0:T(8,128)(2,1)}, bf16[384,512]{1,0:T(8,128)(2,1)}, u32[]{:S(2)}, u32[]{:S(2)}) collective-permute-start(bf16[384,512]{1,0:T(8,128)(2,1)} %get-tuple-element.12.refs_7_), channel_id=1, source_target_pairs={{0,1},{1,0},{2,3},{3,2},{4,5},{5,4},{6,7},{7,6},{8,9},{9,8},{10,11... | collective-permute-start | bytes 1179656 | tf_op jit(solution)/shard_map/ppermute | solution.py:27
  19.8 44.4 %collective-permute-start.11 = (bf16[384,512]{1,0:T(8,128)(2,1)}, bf16[384,512]{1,0:T(8,128)(2,1)}, u32[]{:S(2)}, u32[]{:S(2)}) collective-permute-start(bf16[384,512]{1,0:T(8,128)(2,1)} %get-tuple-element.12.refs_7_), channel_id=1, source_target_pairs={{0,7},{1,2},{2,1},{3,4},{4,3},{5,6},{6,5},{7,0},{8,15},{9,10},{10,... | collective-permute-start | bytes 1179656 | tf_op jit(solution)/shard_map/ppermute | solution.py:28
  27.9 19.3 %collective-permute-start.5 = (bf16[464,512]{1,0:T(8,128)(2,1)S(1)}, bf16[464,512]{1,0:T(8,128)(2,1)}, u32[]{:S(2)}, u32[]{:S(2)}) collective-permute-start(bf16[464,512]{1,0:T(8,128)(2,1)S(1)} %collective-permute-done.4.refs_2_), channel_id=1, source_target_pairs={{0,1},{1,0},{2,3},{3,2},{4,5},{5,4},{6,7},{7,6},{8,9},{9,8},{10,11... | collective-permute-start | bytes 1425416 | tf_op jit(solution)/shard_map/ppermute | solution.py:27
  30.5 21.9 %all-to-all-start = ((bf16[32,24,128]{2,1,0:T(8,128)(2,1)}), bf16[32,24,128]{2,1,0:T(8,128)(2,1)}, u32[]{:S(2)}, u32[]{:S(2)}) async-start(bf16[32,24,128]{2,1,0:T(8,128)(2,1)} %dynamic-slice_bitcast_fusion), calls=%async_computation | async-start | bytes 393216 | tf_op jit(solution)/shard_map/all_to_all | solution.py:331
  40.3 26.5 %collective-permute-start.1 = (bf16[384,512]{1,0:T(8,128)(2,1)}, bf16[384,512]{1,0:T(8,128)(2,1)}, u32[]{:S(2)}, u32[]{:S(2)}) collective-permute-start(bf16[384,512]{1,0:T(8,128)(2,1)} %collective-permute-done.refs_8_), channel_id=1, source_target_pairs={{0,7},{1,2},{2,1},{3,4},{4,3},{5,6},{6,5},{7,0},{8,15},{9,10},{10,... | collective-permute-start | bytes 1179656 | tf_op jit(solution)/shard_map/ppermute | solution.py:28
  45.2 31.8 %collective-permute-start.9 = (bf16[464,512]{1,0:T(8,128)(2,1)S(1)}, bf16[464,512]{1,0:T(8,128)(2,1)}, u32[]{:S(2)}, u32[]{:S(2)}) collective-permute-start(bf16[464,512]{1,0:T(8,128)(2,1)S(1)} %collective-permute-done.8.refs_1_), channel_id=1, source_target_pairs={{0,7},{1,2},{2,1},{3,4},{4,3},{5,6},{6,5},{7,0},{8,15},{9,10},{10,... | collective-permute-start | bytes 1425416 | tf_op jit(solution)/shard_map/ppermute | solution.py:28
  47.1 32.1 %collective-permute-start.6 = (bf16[464,512]{1,0:T(8,128)(2,1)}, bf16[464,512]{1,0:T(8,128)(2,1)}, u32[]{:S(2)}, u32[]{:S(2)}) collective-permute-start(bf16[464,512]{1,0:T(8,128)(2,1)} %collective-permute-done.5.refs_3_), channel_id=1, source_target_pairs={{0,7},{1,2},{2,1},{3,4},{4,3},{5,6},{6,5},{7,0},{8,15},{9,10},{10,... | collective-permute-start | bytes 1425416 | tf_op jit(solution)/shard_map/ppermute | solution.py:28
  52.4 46.6 %copy-start.2 = (bf16[464,512]{1,0:T(8,128)(2,1)S(1)}, bf16[464,512]{1,0:T(8,128)(2,1)}, u32[]{:S(2)}) copy-start(bf16[464,512]{1,0:T(8,128)(2,1)} %get-tuple-element.13.refs_0_) | copy-start | bytes 1425412
  54.9 35.2 %all-to-all-start.1 = ((bf16[32,24,256]{2,1,0:T(8,128)(2,1)}), bf16[32,24,256]{2,1,0:T(8,128)(2,1)}, u32[]{:S(2)}, u32[]{:S(2)}) async-start(bf16[32,24,256]{2,1,0:T(8,128)(2,1)} %broadcast_in_dim.10), calls=%async_computation.1 | async-start | bytes 786432 | tf_op jit(solution)/shard_map/all_to_all | solution.py:42
  64.2 10.8 %collective-permute-start.12 = (bf16[384,512]{1,0:T(8,128)(2,1)}, bf16[384,512]{1,0:T(8,128)(2,1)}, u32[]{:S(2)}, u32[]{:S(2)}) collective-permute-start(bf16[384,512]{1,0:T(8,128)(2,1)} %collective-permute-done.11.refs_9_), channel_id=1, source_target_pairs={{0,1},{1,0},{2,3},{3,2},{4,5},{5,4},{6,7},{7,6},{8,9},{9,8},{10,11... | collective-permute-start | bytes 1179656 | tf_op jit(solution)/shard_map/ppermute | solution.py:27
  66.9 16.6 %collective-permute-start.2 = (bf16[384,512]{1,0:T(8,128)(2,1)}, bf16[384,512]{1,0:T(8,128)(2,1)}, u32[]{:S(2)}, u32[]{:S(2)}) collective-permute-start(bf16[384,512]{1,0:T(8,128)(2,1)} %collective-permute-done.1.refs_11_), channel_id=1, source_target_pairs={{0,1},{1,0},{2,3},{3,2},{4,5},{5,4},{6,7},{7,6},{8,9},{9,8},{10,11... | collective-permute-start | bytes 1179656 | tf_op jit(solution)/shard_map/ppermute | solution.py:27
  75.0 27.1 %collective-permute-start.13 = (bf16[384,512]{1,0:T(8,128)(2,1)}, bf16[384,512]{1,0:T(8,128)(2,1)}, u32[]{:S(2)}, u32[]{:S(2)}) collective-permute-start(bf16[384,512]{1,0:T(8,128)(2,1)} %collective-permute-done.12.refs_10_), channel_id=1, source_target_pairs={{0,7},{1,2},{2,1},{3,4},{4,3},{5,6},{6,5},{7,0},{8,15},{9,10},{10,... | collective-permute-start | bytes 1179656 | tf_op jit(solution)/shard_map/ppermute | solution.py:28
  77.0 22.1 %collective-permute-start.10 = (bf16[464,512]{1,0:T(8,128)(2,1)}, bf16[464,512]{1,0:T(8,128)(2,1)}, u32[]{:S(2)}, u32[]{:S(2)}) collective-permute-start(bf16[464,512]{1,0:T(8,128)(2,1)} %collective-permute-done.9.refs_4_), channel_id=1, source_target_pairs={{0,1},{1,0},{2,3},{3,2},{4,5},{5,4},{6,7},{7,6},{8,9},{9,8},{10,11... | collective-permute-start | bytes 1425416 | tf_op jit(solution)/shard_map/ppermute | solution.py:27
  79.2 26.8 %collective-permute-start.7 = (bf16[464,512]{1,0:T(8,128)(2,1)}, bf16[464,512]{1,0:T(8,128)(2,1)}, u32[]{:S(2)}, u32[]{:S(2)}) collective-permute-start(bf16[464,512]{1,0:T(8,128)(2,1)} %collective-permute-done.6.refs_6_), channel_id=1, source_target_pairs={{0,1},{1,0},{2,3},{3,2},{4,5},{5,4},{6,7},{7,6},{8,9},{9,8},{10,11... | collective-permute-start | bytes 1425416 | tf_op jit(solution)/shard_map/ppermute | solution.py:32
  83.5 25.3 %collective-permute-start.3 = (bf16[384,512]{1,0:T(8,128)(2,1)}, bf16[384,512]{1,0:T(8,128)(2,1)}, u32[]{:S(2)}, u32[]{:S(2)}) collective-permute-start(bf16[384,512]{1,0:T(8,128)(2,1)} %collective-permute-done.2.refs_12_), channel_id=1, source_target_pairs={{0,7},{1,2},{2,1},{3,4},{4,3},{5,6},{6,5},{7,0},{8,15},{9,10},{10,... | collective-permute-start | bytes 1179656 | tf_op jit(solution)/shard_map/ppermute | solution.py:33
  90.2 12.0 %copy-start.7 = (s32[8]{0:T(128)S(1)}, s32[8]{0:T(128)}, u32[]{:S(2)}) copy-start(s32[8]{0:T(128)} %and_select_fusion.1.owner_ref) | copy-start | bytes 100
  99.0 3.2 %copy-start.4 = (bf16[384,512]{1,0:T(8,128)(2,1)S(1)}, bf16[384,512]{1,0:T(8,128)(2,1)}, u32[]{:S(2)}) copy-start(bf16[384,512]{1,0:T(8,128)(2,1)} %get-tuple-element.12.refs_7_) | copy-start | bytes 1179652
  99.1 0.7 copy-start.6
  102.2 3.9 %copy-start.3 = (s32[256,4]{1,0:T(8,128)S(1)}, s32[256,4]{1,0:T(8,128)}, u32[]{:S(2)}) copy-start(s32[256,4]{1,0:T(8,128)} %copy.22.ids_ref) | copy-start | bytes 12292
  110.4 24.5 %copy-start.5 = (s32[256]{0:T(256)S(1)}, s32[256]{0:T(256)}, u32[]{:S(2)}) copy-start(s32[256]{0:T(256)} %param.20) | copy-start | bytes 3076
  110.4 24.5 %copy-start.8 = (s32[256,3]{0,1:T(4,128)S(1)}, s32[256,3]{0,1:T(4,128)}, u32[]{:S(2)}) copy-start(s32[256,3]{0,1:T(4,128)} %param.21) | copy-start | bytes 9220
  120.9 14.1 %all-to-all-start.3 = ((f32[8,1,3072]{2,1,0:T(1,128)}), f32[8,1,3072]{2,1,0:T(1,128)S(1)}, u32[]{:S(2)}, u32[]{:S(2)}) async-start(f32[8,1,3072]{2,1,0:T(1,128)} %shard_map.128), calls=%async_computation.3 | async-start | bytes 196608 | tf_op jit(solution)/shard_map/all_to_all | solution.py:395
where the time goes:
time: 137 us; the launch traced here: 136 us
  starting transfers between devices  74.4 us (54%)
  blocking collectives  21.8 us (16%)
  Pallas kernels  16 us (12%)
  waiting for transfers between devices  11.2 us (8%)
  local copies, waits for them, and re-layouts  6.37 us (5%)
  other arithmetic  4.16 us (3%)
    ppermute x6, starting transfers between devices, ring(): two = lax.ppermute(one, axis, odd)  26.7 us
    ppermute x6, starting transfers between devices, ring(): came = lax.ppermute(two, axis, even)  14.7 us
    pallas_call x7, Pallas kernels, call(): pl.pallas_call(body, out_shape=out_shape, in_specs=[smem] * (scalars is n...  13.6 us
    all_to_all x1, starting transfers between devices, one_device(): lax.all_to_all(pieces, CHIPS, split_axis=0, concat_axis=0, tiled=True)  9.79 us
    all_to_all x1, blocking collectives, one_device(): stats = lax.all_to_all(stats, near, split_axis=0, concat_axis=0, tiled=True)  9.69 us
    all_to_all x1, starting transfers between devices, copy_for_each(): return lax.all_to_all(copies, axis, split_axis=0, concat_axis=0, tiled=True)  9.27 us
    all_gather x1, blocking collectives, one_device(): turned = lax.all_gather(turned, CORE)  8.87 us
    all_to_all x1, waiting for transfers between devices, one_device(): lax.all_to_all(stats, VOCAB[0], split_axis=0, concat_axis=0, tiled=True)  7.04 us
  transfers between devices with their start and end apart: 17, of which 2 were waited for; matrix products, arithmetic and copies ran while one was open for 8% of the time, Pallas kernels for 8%

commit v1 on v0

--- a/solution.py
+++ b/solution.py
@@ -114,21 +114,10 @@
     return tall, row // block.shape[0] == owner
 
 
-def part_kernel(h, owner_ref, hidden_ref, *refs):
-    *refs, head_ref = refs
-    count = h.count - 1
-    head = None
-    for k in range(count):
-        for low, block in ((0, refs[k][h.head_at :, :]), (h.rest, refs[count + k][...])):
-            at = pl.multiple_of(owner_ref[k] * h.head + low, 128)
-            term = dot(hidden_ref[:, pl.ds(at, block.shape[0])], block)
-            head = term if head is None else head + term
-    head_ref[...] = head
-
-
-def lift_kernel(h, owner_ref, turned_ref, *refs):
+def part_kernel(h, owner_ref, turned_ref, hidden_ref, *refs):
     shard_refs = refs[: h.count - 1]
-    proj_ref, one_ref, two_ref, three_ref, wide_ref = refs[h.count - 1 :]
+    other_refs = refs[h.count - 1 : 2 * h.count - 2]
+    proj_ref, head_ref, one_ref, two_ref, three_ref, wide_ref = refs[2 * h.count - 2 :]
     proj_ref[...] = turned_ref[...].T
     n, half = h.count, h.half
     last = owner_ref[n - 1]
@@ -138,7 +127,8 @@
         wide_ref[side, pl.ds(pl.multiple_of(last * h.one, h.one), h.one), :] = blank
         two_ref[side, pl.ds(pl.multiple_of(last * h.two, h.two), h.two), :] = small
     threes = [jnp.zeros((h.three * n, half), jnp.float32)] * 2
-    for k, ref in enumerate(shard_refs):
+    head = None
+    for k, (ref, other) in enumerate(zip(shard_refs, other_refs)):
         owner = owner_ref[k]
         for side in range(2):
             wide_ref[side, pl.ds(pl.multiple_of(owner * h.one, h.one), h.one), :] = ref[
@@ -152,6 +142,11 @@
         for side in range(2):
             tall, there = spread(both[side * h.three : (side + 1) * h.three], owner, n)
             threes[side] = jnp.where(there, tall, threes[side])
+        for low, block in ((0, ref[h.head_at :, :]), (h.rest, other[...])):
+            at = pl.multiple_of(owner * h.head + low, 128)
+            term = dot(hidden_ref[:, pl.ds(at, block.shape[0])], block)
+            head = term if head is None else head + term
+    head_ref[...] = head
     for side in range(2):
         three_ref[side] = threes[side].astype(three_ref.dtype)
         one_ref[:, side * half : (side + 1) * half] = dot(
@@ -341,22 +336,18 @@
     wide = jnp.bfloat16
     part_call = kernel_call(
         functools.partial(part_kernel, h),
-        jax.ShapeDtypeStruct((rows, head_cols), jnp.float32),
-        2 * rows * head_weight.size * n_grp,
-    )
-    head_part = part_call(owners, hidden, shard, *found, other, *others)
-    lift_call = kernel_call(
-        functools.partial(lift_kernel, h),
         (
             jax.ShapeDtypeStruct((rows, turned.shape[0]), wide),
+            jax.ShapeDtypeStruct((rows, head_cols), jnp.float32),
             jax.ShapeDtypeStruct((rows, tail_cols), jnp.float32),
             jax.ShapeDtypeStruct((2, h.two * n_grp, half), wide),
             jax.ShapeDtypeStruct((2, h.three * n_grp, half), wide),
         ),
-        2 * rows * tail_one.size * n_grp,
+        2 * rows * (shard.size + other.size) * n_grp,
         [pltpu.VMEM((2, h.one * n_grp, half), wide)],
-    )
-    proj, one_part, *small_rows = lift_call(owners, turned, shard, *found)
+        mib=16,
+    )
+    part = part_call(owners, turned, hidden, shard, *found, other, *others)
 
     cluster_logits = dot(hidden, cluster_weight)
     relative = targets - V_HEAD
@@ -379,9 +370,8 @@
         2 * rows * shard.size,
         [pltpu.VMEM((2, h.two * n_grp, half), wide)],
     )
-    table, head_part = tails_call(
-        owners, first, hidden, proj, head_part, one_part, *small_rows, ids
-    )
+    proj, head_part, *tail_parts = part
+    table, head_part = tails_call(owners, first, hidden, proj, head_part, *tail_parts, ids)
     stats = kernel_call(
         functools.partial(last_kernel, h),
         jax.ShapeDtypeStruct((n_near, 1, 12 * rows), jnp.float32),

time: 137 us -> 129 us (0.942)
  starting transfers between devices: 74.4 us -> 70.4 us
  local copies, waits for them, and re-layouts: 6.37 us -> 3.01 us
  waiting for transfers between devices: 11.2 us -> 14.4 us
  other arithmetic: 4.16 us -> 1.02 us
  Pallas kernels: 16 us -> 13.4 us
  blocking collectives: 21.8 us -> 24.1 us
    all_to_all x1, waiting for transfers between devices: 0.01 us -> 3.08 us  [one_device(): lax.all_to_all(pieces, CHIPS, split_axis=0, concat_axis=0, tiled=True)]
    all_to_all x1, starting transfers between devices: 9.27 us -> 6.27 us  [copy_for_each(): return lax.all_to_all(copies, axis, split_axis=0, concat_axis=0, tiled=True)]
    ppermute x6, starting transfers between devices: 26.7 us -> 29.3 us  [ring(): two = lax.ppermute(one, axis, odd)]
    pallas_call x7 -> x6, Pallas kernels: 13.6 us -> 11 us  [call(): pl.pallas_call(body, out_shape=out_shape, in_specs=[smem] * (scalars is n...]
    all_to_all x1, blocking collectives: 9.69 us -> 12 us  [one_device(): stats = lax.all_to_all(stats, near, split_axis=0, concat_axis=0, tiled=True)]
    ppermute x6, starting transfers between devices: 14.7 us -> 13 us  [ring(): came = lax.ppermute(two, axis, even)]
  transfers between devices with their start and end apart: 17 -> 17, of which waited for: 2 -> 4; matrix products, arithmetic and copies ran while one was open for 8% -> 3% of each run, Pallas kernels for 8% -> 6%
where the time goes in v1:
time: 129 us; the launch traced here: 128 us
  starting transfers between devices  70.4 us (55%)
  blocking collectives  24.1 us (19%)
  waiting for transfers between devices  14.4 us (11%)
  Pallas kernels  13.4 us (10%)
  local copies, waits for them, and re-layouts  3.01 us (2%)
    ppermute x6, starting transfers between devices, ring(): two = lax.ppermute(one, axis, odd)  29.3 us
    ppermute x6, starting transfers between devices, ring(): came = lax.ppermute(two, axis, even)  13 us
    all_to_all x1, blocking collectives, one_device(): stats = lax.all_to_all(stats, near, split_axis=0, concat_axis=0, tiled=True)  12 us
    pallas_call x6, Pallas kernels, call(): pl.pallas_call(body, out_shape=out_shape, in_specs=[smem] * (scalars is n...  11 us
    all_to_all x1, starting transfers between devices, one_device(): lax.all_to_all(pieces, CHIPS, split_axis=0, concat_axis=0, tiled=True)  9.67 us
    all_gather x1, blocking collectives, one_device(): turned = lax.all_gather(turned, CORE)  8.97 us
    all_to_all x1, waiting for transfers between devices, one_device(): lax.all_to_all(stats, VOCAB[0], split_axis=0, concat_axis=0, tiled=True)  7.04 us
    all_to_all x1, starting transfers between devices, one_device(): lax.all_to_all(stats, VOCAB[0], split_axis=0, concat_axis=0, tiled=True)  6.38 us
  transfers between devices with their start and end apart: 17, of which 4 were waited for; matrix products, arithmetic and copies ran while one was open for 3% of the time, Pallas kernels for 6%

profile of v1, /device:TPU:1, one launch (start us, length us, event | category | flops | bytes accessed | tf_op | source)
XLA Modules:
  0.0 128.0 jit_solution(656300998605864417)
XLA Ops:
  0.6 0.0 copy-start
  0.6 0.0 copy-start.1
  0.7 2.4 %shard_map.122 = (bf16[464,512]{1,0:T(8,128)(2,1)}, bf16[384,512]{1,0:T(8,128)(2,1)}) custom-call(bf16[128,1024]{1,0:T(8,128)(2,1)} %refs_0_.1, bf16[32,1024]{1,0:T(8,128)(2,1)} %refs_1_.1, bf16[8,1024]{1,0:T(8,128)(2,1)} %refs_2_.1, bf16[512,512]{1,0:T(8,128)(2,1)} %refs_3_.1), custom_call_target="tpu_custom_call" | custom-call | tf_op jit(solution)/shard_map/pallas_call | solution.py:92
  3.0 11.5 %collective-permute-start.4 = (bf16[464,512]{1,0:T(8,128)(2,1)}, bf16[464,512]{1,0:T(8,128)(2,1)S(1)}, u32[]{:S(2)}, u32[]{:S(2)}) collective-permute-start(bf16[464,512]{1,0:T(8,128)(2,1)} %get-tuple-element.14.refs_0_), channel_id=1, source_target_pairs={{0,7},{1,2},{2,1},{3,4},{4,3},{5,6},{6,5},{7,0},{8,15},{9,10},{10,... | collective-permute-start | bytes 1425416 | tf_op jit(solution)/shard_map/ppermute | solution.py:28
  14.5 1.9 %collective-permute-start.8 = (bf16[464,512]{1,0:T(8,128)(2,1)}, bf16[464,512]{1,0:T(8,128)(2,1)}, u32[]{:S(2)}, u32[]{:S(2)}) collective-permute-start(bf16[464,512]{1,0:T(8,128)(2,1)} %get-tuple-element.14.refs_0_), channel_id=1, source_target_pairs={{0,1},{1,0},{2,3},{3,2},{4,5},{5,4},{6,7},{7,6},{8,9},{9,8},{10,11... | collective-permute-start | bytes 1425416 | tf_op jit(solution)/shard_map/ppermute | solution.py:27
  16.5 3.4 %collective-permute-start = (bf16[384,512]{1,0:T(8,128)(2,1)}, bf16[384,512]{1,0:T(8,128)(2,1)}, u32[]{:S(2)}, u32[]{:S(2)}) collective-permute-start(bf16[384,512]{1,0:T(8,128)(2,1)} %get-tuple-element.13.refs_7_), channel_id=1, source_target_pairs={{0,1},{1,0},{2,3},{3,2},{4,5},{5,4},{6,7},{7,6},{8,9},{9,8},{10,11... | collective-permute-start | bytes 1179656 | tf_op jit(solution)/shard_map/ppermute | solution.py:27
  19.8 1.9 %collective-permute-start.11 = (bf16[384,512]{1,0:T(8,128)(2,1)}, bf16[384,512]{1,0:T(8,128)(2,1)}, u32[]{:S(2)}, u32[]{:S(2)}) collective-permute-start(bf16[384,512]{1,0:T(8,128)(2,1)} %get-tuple-element.13.refs_7_), channel_id=1, source_target_pairs={{0,7},{1,2},{2,1},{3,4},{4,3},{5,6},{6,5},{7,0},{8,15},{9,10},{10,... | collective-permute-start | bytes 1179656 | tf_op jit(solution)/shard_map/ppermute | solution.py:28
  21.8 1.0 pad_maximum_fusion
  22.7 3.2 %all_gather.9 = bf16[128,1344]{1,0:T(8,128)(2,1)S(1)} all-gather(bf16[64,1344]{1,0:T(8,128)(2,1)S(1)} %pad_maximum_fusion), channel_id=1, replica_groups=mesh['vocab_0'=8,'vocab_1'=4,'vocab_2'=2,'grp'=8] {'vocab_2'}, dimensions={0}, use_global_device_ids=true | all-gather | bytes 516096 | tf_op jit(solution)/shard_map/all_gather | solution.py:320
  25.9 0.2 copy.21
  26.2 0.0 collective-permute-done.4.refs_2_
  26.2 1.9 %collective-permute-start.5 = (bf16[464,512]{1,0:T(8,128)(2,1)S(1)}, bf16[464,512]{1,0:T(8,128)(2,1)}, u32[]{:S(2)}, u32[]{:S(2)}) collective-permute-start(bf16[464,512]{1,0:T(8,128)(2,1)S(1)} %collective-permute-done.4.refs_2_), channel_id=1, source_target_pairs={{0,1},{1,0},{2,3},{3,2},{4,5},{5,4},{6,7},{7,6},{8,9},{9,8},{10,11... | collective-permute-start | bytes 1425416 | tf_op jit(solution)/shard_map/ppermute | solution.py:27
  28.1 0.0 copy-start.4
  28.2 0.7 dynamic-slice_bitcast_fusion
  28.9 9.7 %all-to-all-start = ((bf16[32,24,128]{2,1,0:T(8,128)(2,1)}), bf16[32,24,128]{2,1,0:T(8,128)(2,1)S(1)}, u32[]{:S(2)}, u32[]{:S(2)}) async-start(bf16[32,24,128]{2,1,0:T(8,128)(2,1)} %dynamic-slice_bitcast_fusion), calls=%async_computation | async-start | bytes 393216 | tf_op jit(solution)/shard_map/all_to_all | solution.py:326
  38.5 0.0 collective-permute-done.refs_8_
  38.6 4.9 %collective-permute-start.1 = (bf16[384,512]{1,0:T(8,128)(2,1)}, bf16[384,512]{1,0:T(8,128)(2,1)}, u32[]{:S(2)}, u32[]{:S(2)}) collective-permute-start(bf16[384,512]{1,0:T(8,128)(2,1)} %collective-permute-done.refs_8_), channel_id=1, source_target_pairs={{0,7},{1,2},{2,1},{3,4},{4,3},{5,6},{6,5},{7,0},{8,15},{9,10},{10,... | collective-permute-start | bytes 1179656 | tf_op jit(solution)/shard_map/ppermute | solution.py:28
  43.4 0.0 collective-permute-done.8.refs_1_
  43.4 1.9 %collective-permute-start.9 = (bf16[464,512]{1,0:T(8,128)(2,1)}, bf16[464,512]{1,0:T(8,128)(2,1)}, u32[]{:S(2)}, u32[]{:S(2)}) collective-permute-start(bf16[464,512]{1,0:T(8,128)(2,1)} %collective-permute-done.8.refs_1_), channel_id=1, source_target_pairs={{0,7},{1,2},{2,1},{3,4},{4,3},{5,6},{6,5},{7,0},{8,15},{9,10},{10,... | collective-permute-start | bytes 1425416 | tf_op jit(solution)/shard_map/ppermute | solution.py:28
  45.4 0.0 copy-start.2
  45.4 3.1 %all-to-all-done.weight_ref = bf16[32,24,128]{2,1,0:T(8,128)(2,1)S(1)} async-done(((bf16[32,24,128]{2,1,0:T(8,128)(2,1)}), bf16[32,24,128]{2,1,0:T(8,128)(2,1)S(1)}, u32[]{:S(2)}, u32[]{:S(2)}) %all-to-all-start) | async-done | bytes 196640 | tf_op jit(solution)/shard_map/all_to_all | solution.py:326
  48.5 0.0 copy-done.1
  48.5 0.7 shard_map.123
  49.2 0.8 broadcast_in_dim.10
  50.0 6.3 %all-to-all-start.1 = ((bf16[32,24,256]{2,1,0:T(8,128)(2,1)}), bf16[32,24,256]{2,1,0:T(8,128)(2,1)}, u32[]{:S(2)}, u32[]{:S(2)}) async-start(bf16[32,24,256]{2,1,0:T(8,128)(2,1)} %broadcast_in_dim.10), calls=%async_computation.1 | async-start | bytes 786432 | tf_op jit(solution)/shard_map/all_to_all | solution.py:42
  56.2 0.0 collective-permute-done.11.refs_9_
  56.3 1.9 %collective-permute-start.12 = (bf16[384,512]{1,0:T(8,128)(2,1)}, bf16[384,512]{1,0:T(8,128)(2,1)}, u32[]{:S(2)}, u32[]{:S(2)}) collective-permute-start(bf16[384,512]{1,0:T(8,128)(2,1)} %collective-permute-done.11.refs_9_), channel_id=1, source_target_pairs={{0,1},{1,0},{2,3},{3,2},{4,5},{5,4},{6,7},{7,6},{8,9},{9,8},{10,11... | collective-permute-start | bytes 1179656 | tf_op jit(solution)/shard_map/ppermute | solution.py:27
  58.2 0.0 collective-permute-done.5.refs_3_
  58.2 4.8 %collective-permute-start.6 = (bf16[464,512]{1,0:T(8,128)(2,1)}, bf16[464,512]{1,0:T(8,128)(2,1)}, u32[]{:S(2)}, u32[]{:S(2)}) collective-permute-start(bf16[464,512]{1,0:T(8,128)(2,1)} %collective-permute-done.5.refs_3_), channel_id=1, source_target_pairs={{0,7},{1,2},{2,1},{3,4},{4,3},{5,6},{6,5},{7,0},{8,15},{9,10},{10,... | collective-permute-start | bytes 1425416 | tf_op jit(solution)/shard_map/ppermute | solution.py:28
  63.0 0.0 copy-done.4
  63.1 0.1 stack.42
  63.1 0.0 collective-permute-done.1.refs_11_
  63.1 1.9 %collective-permute-start.2 = (bf16[384,512]{1,0:T(8,128)(2,1)}, bf16[384,512]{1,0:T(8,128)(2,1)}, u32[]{:S(2)}, u32[]{:S(2)}) collective-permute-start(bf16[384,512]{1,0:T(8,128)(2,1)} %collective-permute-done.1.refs_11_), channel_id=1, source_target_pairs={{0,1},{1,0},{2,3},{3,2},{4,5},{5,4},{6,7},{7,6},{8,9},{9,8},{10,11... | collective-permute-start | bytes 1179656 | tf_op jit(solution)/shard_map/ppermute | solution.py:27
  65.1 1.7 %collective-permute-done.12.refs_10_ = bf16[384,512]{1,0:T(8,128)(2,1)} collective-permute-done((bf16[384,512]{1,0:T(8,128)(2,1)}, bf16[384,512]{1,0:T(8,128)(2,1)}, u32[]{:S(2)}, u32[]{:S(2)}) %collective-permute-start.12) | collective-permute-done | bytes 393248 | tf_op jit(solution)/shard_map/ppermute | solution.py:27
  66.8 4.3 %collective-permute-start.13 = (bf16[384,512]{1,0:T(8,128)(2,1)}, bf16[384,512]{1,0:T(8,128)(2,1)}, u32[]{:S(2)}, u32[]{:S(2)}) collective-permute-start(bf16[384,512]{1,0:T(8,128)(2,1)} %collective-permute-done.12.refs_10_), channel_id=1, source_target_pairs={{0,7},{1,2},{2,1},{3,4},{4,3},{5,6},{6,5},{7,0},{8,15},{9,10},{10,... | collective-permute-start | bytes 1179656 | tf_op jit(solution)/shard_map/ppermute | solution.py:28
  71.1 0.0 collective-permute-done.9.refs_4_
  71.1 1.9 %collective-permute-start.10 = (bf16[464,512]{1,0:T(8,128)(2,1)}, bf16[464,512]{1,0:T(8,128)(2,1)}, u32[]{:S(2)}, u32[]{:S(2)}) collective-permute-start(bf16[464,512]{1,0:T(8,128)(2,1)} %collective-permute-done.9.refs_4_), channel_id=1, source_target_pairs={{0,1},{1,0},{2,3},{3,2},{4,5},{5,4},{6,7},{7,6},{8,9},{9,8},{10,11... | collective-permute-start | bytes 1425416 | tf_op jit(solution)/shard_map/ppermute | solution.py:27
  73.1 2.5 %collective-permute-done.2.refs_12_ = bf16[384,512]{1,0:T(8,128)(2,1)} collective-permute-done((bf16[384,512]{1,0:T(8,128)(2,1)}, bf16[384,512]{1,0:T(8,128)(2,1)}, u32[]{:S(2)}, u32[]{:S(2)}) %collective-permute-start.2) | collective-permute-done | bytes 393248 | tf_op jit(solution)/shard_map/ppermute | solution.py:27
  75.6 3.9 %collective-permute-start.3 = (bf16[384,512]{1,0:T(8,128)(2,1)}, bf16[384,512]{1,0:T(8,128)(2,1)}, u32[]{:S(2)}, u32[]{:S(2)}) collective-permute-start(bf16[384,512]{1,0:T(8,128)(2,1)} %collective-permute-done.2.refs_12_), channel_id=1, source_target_pairs={{0,7},{1,2},{2,1},{3,4},{4,3},{5,6},{6,5},{7,0},{8,15},{9,10},{10,... | collective-permute-start | bytes 1179656 | tf_op jit(solution)/shard_map/ppermute | solution.py:33
  79.6 0.0 collective-permute-done.6.refs_6_
  79.6 1.9 %collective-permute-start.7 = (bf16[464,512]{1,0:T(8,128)(2,1)}, bf16[464,512]{1,0:T(8,128)(2,1)}, u32[]{:S(2)}, u32[]{:S(2)}) collective-permute-start(bf16[464,512]{1,0:T(8,128)(2,1)} %collective-permute-done.6.refs_6_), channel_id=1, source_target_pairs={{0,1},{1,0},{2,3},{3,2},{4,5},{5,4},{6,7},{7,6},{8,9},{9,8},{10,11... | collective-permute-start | bytes 1425416 | tf_op jit(solution)/shard_map/ppermute | solution.py:32
  81.5 0.1 copy.22.ids_ref
  81.7 0.0 all-to-all-done.1
  81.7 9.0 %all-gather = bf16[64,24,256]{2,1,0:T(8,128)(2,1)S(1)} all-gather(bf16[32,24,256]{2,1,0:T(8,128)(2,1)} %all-to-all-done.1), channel_id=2, replica_groups=mesh['vocab_0'=8,'vocab_1'=4,'vocab_2'=2,'grp'=8] {'vocab_2'}, dimensions={0}, use_global_device_ids=true | all-gather | bytes 1179648 | tf_op jit(solution)/shard_map/all_gather | solution.py:333
  90.6 0.0 collective-permute-done.13.refs_13_
  90.6 0.0 collective-permute-done.10.refs_5_
  90.6 0.0 copy-done.2
  90.6 0.0 copy-start.3
  90.7 1.0 copy-done.3
  91.6 4.6 %shard_map.124 = (bf16[256,1536]{1,0:T(8,128)(2,1)S(1)}, f32[256,512]{1,0:T(8,128)S(1)}, f32[256,1024]{1,0:T(8,128)S(1)}, bf16[2,256,512]{2,1,0:T(8,128)(2,1)S(1)}, bf16[2,64,512]{2,1,0:T(8,128)(2,1)S(1)}) custom-call(s32[8]{0:T(128)S(1)} %and_select_fusion.1.owner_ref, bf16[1536,256]{1,0:T(8,128)(2,1)S(1)} %bitcast.21, bf16[256,4096]{1,0:T(8,128)(2,1)S(1)} %copy-done.1, ...), custom_call_target="tpu_custom_call" | custom-call | flops 1778384896 | bytes 1048576 | tf_op jit(solution)/shard_map/pallas_call | solution.py:54
  96.2 0.0 collective-permute-done.7.first_ref
  96.3 2.8 %shard_map.125 = (f32[256,128]{1,0:T(8,128)S(1)}, f32[256,512]{1,0:T(8,128)S(1)}) custom-call(s32[8]{0:T(128)S(1)} %and_select_fusion.1.owner_ref, bf16[464,512]{1,0:T(8,128)(2,1)} %collective-permute-done.7.first_ref, bf16[256,4096]{1,0:T(8,128)(2,1)S(1)} %copy-done.1, bf16[256,1536]{1,0:T(8,128)(2,1)S(1)} %get-tuple-element.15.proj_ref, ...), custom_call_target="tpu_custom_call" | custom-call | flops 121634816 | bytes 1048576 | tf_op jit(solution)/shard_map/pallas_call | solution.py:54
  99.0 0.0 collective-permute-done.3.second_ref
  99.0 1.6 %shard_map.126 = f32[8,1,3072]{2,1,0:T(1,128)S(1)} custom-call(s32[8]{0:T(128)S(1)} %and_select_fusion.1.owner_ref, bf16[384,512]{1,0:T(8,128)(2,1)} %collective-permute-done.3.second_ref, bf16[256,4096]{1,0:T(8,128)(2,1)S(1)} %copy-done.1, f32[256,512]{1,0:T(8,128)S(1)} %get-tuple-element.20.head_ref, f32[256,128]{1,0:T(8,128)S(1)} %get-tuple-element.21.table_ref, ...), custom_call_target="tpu_custom_call" | custom-call | flops 100663296 | bytes 1048576 | tf_op jit(solution)/shard_map/pallas_call | solution.py:54
  100.6 0.0 copy-start.5
  100.6 12.0 %all_to_all.20.stats_ref = f32[8,1,3072]{2,1,0:T(1,128)S(1)} all-to-all(f32[8,1,3072]{2,1,0:T(1,128)S(1)} %shard_map.126), channel_id=1, replica_groups=mesh['vocab_0'=8,'vocab_1'=4,'vocab_2'=2,'grp'=8] {'vocab_1','vocab_2'}, dimensions={0} | all-to-all | bytes 196608 | tf_op jit(solution)/shard_map/all_to_all | solution.py:381
  112.6 0.7 shard_map.127
  113.3 6.4 %all-to-all-start.3 = ((f32[8,1,3072]{2,1,0:T(1,128)}), f32[8,1,3072]{2,1,0:T(1,128)S(1)}, u32[]{:S(2)}, u32[]{:S(2)}) async-start(f32[8,1,3072]{2,1,0:T(1,128)} %shard_map.127), calls=%async_computation.3 | async-start | bytes 196608 | tf_op jit(solution)/shard_map/all_to_all | solution.py:385
  119.7 0.0 copy-done
  119.7 0.6 fusion.1.scores_ref
  120.3 7.0 %all-to-all-done.3.stats_ref = f32[8,1,3072]{2,1,0:T(1,128)S(1)} async-done(((f32[8,1,3072]{2,1,0:T(1,128)}), f32[8,1,3072]{2,1,0:T(1,128)S(1)}, u32[]{:S(2)}, u32[]{:S(2)}) %all-to-all-start.3) | async-done | bytes 98336 | tf_op jit(solution)/shard_map/all_to_all | solution.py:385
  127.4 0.0 copy-done.5
  127.4 0.7 shard_map.128
  (5 shorter events, 0.1 us)
Async XLA Ops:
  0.6 119.1 %copy-start = (bf16[4096,3]{0,1:T(4,128)(2,1)S(1)}, bf16[4096,3]{0,1:T(4,128)(2,1)}, u32[]{:S(2)}) copy-start(bf16[4096,3]{0,1:T(4,128)(2,1)} %param.13) | copy-start | bytes 73732
  0.6 47.8 %copy-start.1 = (bf16[256,4096]{1,0:T(8,128)(2,1)S(1)}, bf16[256,4096]{1,0:T(8,128)(2,1)}, u32[]{:S(2)}) copy-start(bf16[256,4096]{1,0:T(8,128)(2,1)} %hidden_ref.7) | copy-start | bytes 6291460
  3.0 23.2 %collective-permute-start.4 = (bf16[464,512]{1,0:T(8,128)(2,1)}, bf16[464,512]{1,0:T(8,128)(2,1)S(1)}, u32[]{:S(2)}, u32[]{:S(2)}) collective-permute-start(bf16[464,512]{1,0:T(8,128)(2,1)} %get-tuple-element.14.refs_0_), channel_id=1, source_target_pairs={{0,7},{1,2},{2,1},{3,4},{4,3},{5,6},{6,5},{7,0},{8,15},{9,10},{10,... | collective-permute-start | bytes 1425416 | tf_op jit(solution)/shard_map/ppermute | solution.py:28
  14.5 28.9 %collective-permute-start.8 = (bf16[464,512]{1,0:T(8,128)(2,1)}, bf16[464,512]{1,0:T(8,128)(2,1)}, u32[]{:S(2)}, u32[]{:S(2)}) collective-permute-start(bf16[464,512]{1,0:T(8,128)(2,1)} %get-tuple-element.14.refs_0_), channel_id=1, source_target_pairs={{0,1},{1,0},{2,3},{3,2},{4,5},{5,4},{6,7},{7,6},{8,9},{9,8},{10,11... | collective-permute-start | bytes 1425416 | tf_op jit(solution)/shard_map/ppermute | solution.py:27
  16.5 22.1 %collective-permute-start = (bf16[384,512]{1,0:T(8,128)(2,1)}, bf16[384,512]{1,0:T(8,128)(2,1)}, u32[]{:S(2)}, u32[]{:S(2)}) collective-permute-start(bf16[384,512]{1,0:T(8,128)(2,1)} %get-tuple-element.13.refs_7_), channel_id=1, source_target_pairs={{0,1},{1,0},{2,3},{3,2},{4,5},{5,4},{6,7},{7,6},{8,9},{9,8},{10,11... | collective-permute-start | bytes 1179656 | tf_op jit(solution)/shard_map/ppermute | solution.py:27
  19.8 36.4 %collective-permute-start.11 = (bf16[384,512]{1,0:T(8,128)(2,1)}, bf16[384,512]{1,0:T(8,128)(2,1)}, u32[]{:S(2)}, u32[]{:S(2)}) collective-permute-start(bf16[384,512]{1,0:T(8,128)(2,1)} %get-tuple-element.13.refs_7_), channel_id=1, source_target_pairs={{0,7},{1,2},{2,1},{3,4},{4,3},{5,6},{6,5},{7,0},{8,15},{9,10},{10,... | collective-permute-start | bytes 1179656 | tf_op jit(solution)/shard_map/ppermute | solution.py:28
  26.2 32.0 %collective-permute-start.5 = (bf16[464,512]{1,0:T(8,128)(2,1)S(1)}, bf16[464,512]{1,0:T(8,128)(2,1)}, u32[]{:S(2)}, u32[]{:S(2)}) collective-permute-start(bf16[464,512]{1,0:T(8,128)(2,1)S(1)} %collective-permute-done.4.refs_2_), channel_id=1, source_target_pairs={{0,1},{1,0},{2,3},{3,2},{4,5},{5,4},{6,7},{7,6},{8,9},{9,8},{10,11... | collective-permute-start | bytes 1425416 | tf_op jit(solution)/shard_map/ppermute | solution.py:27
  28.1 34.9 %copy-start.4 = (s32[256]{0:T(256)S(1)}, s32[256]{0:T(256)}, u32[]{:S(2)}) copy-start(s32[256]{0:T(256)} %param.20) | copy-start | bytes 3076
  28.9 19.6 %all-to-all-start = ((bf16[32,24,128]{2,1,0:T(8,128)(2,1)}), bf16[32,24,128]{2,1,0:T(8,128)(2,1)S(1)}, u32[]{:S(2)}, u32[]{:S(2)}) async-start(bf16[32,24,128]{2,1,0:T(8,128)(2,1)} %dynamic-slice_bitcast_fusion), calls=%async_computation | async-start | bytes 393216 | tf_op jit(solution)/shard_map/all_to_all | solution.py:326
  38.6 24.6 %collective-permute-start.1 = (bf16[384,512]{1,0:T(8,128)(2,1)}, bf16[384,512]{1,0:T(8,128)(2,1)}, u32[]{:S(2)}, u32[]{:S(2)}) collective-permute-start(bf16[384,512]{1,0:T(8,128)(2,1)} %collective-permute-done.refs_8_), channel_id=1, source_target_pairs={{0,7},{1,2},{2,1},{3,4},{4,3},{5,6},{6,5},{7,0},{8,15},{9,10},{10,... | collective-permute-start | bytes 1179656 | tf_op jit(solution)/shard_map/ppermute | solution.py:28
  43.4 27.7 %collective-permute-start.9 = (bf16[464,512]{1,0:T(8,128)(2,1)}, bf16[464,512]{1,0:T(8,128)(2,1)}, u32[]{:S(2)}, u32[]{:S(2)}) collective-permute-start(bf16[464,512]{1,0:T(8,128)(2,1)} %collective-permute-done.8.refs_1_), channel_id=1, source_target_pairs={{0,7},{1,2},{2,1},{3,4},{4,3},{5,6},{6,5},{7,0},{8,15},{9,10},{10,... | collective-permute-start | bytes 1425416 | tf_op jit(solution)/shard_map/ppermute | solution.py:28
  45.4 45.3 %copy-start.2 = (bf16[464,512]{1,0:T(8,128)(2,1)S(1)}, bf16[464,512]{1,0:T(8,128)(2,1)}, u32[]{:S(2)}) copy-start(bf16[464,512]{1,0:T(8,128)(2,1)} %get-tuple-element.14.refs_0_) | copy-start | bytes 1425412
  50.0 31.7 %all-to-all-start.1 = ((bf16[32,24,256]{2,1,0:T(8,128)(2,1)}), bf16[32,24,256]{2,1,0:T(8,128)(2,1)}, u32[]{:S(2)}, u32[]{:S(2)}) async-start(bf16[32,24,256]{2,1,0:T(8,128)(2,1)} %broadcast_in_dim.10), calls=%async_computation.1 | async-start | bytes 786432 | tf_op jit(solution)/shard_map/all_to_all | solution.py:42
  56.3 10.6 %collective-permute-start.12 = (bf16[384,512]{1,0:T(8,128)(2,1)}, bf16[384,512]{1,0:T(8,128)(2,1)}, u32[]{:S(2)}, u32[]{:S(2)}) collective-permute-start(bf16[384,512]{1,0:T(8,128)(2,1)} %collective-permute-done.11.refs_9_), channel_id=1, source_target_pairs={{0,1},{1,0},{2,3},{3,2},{4,5},{5,4},{6,7},{7,6},{8,9},{9,8},{10,11... | collective-permute-start | bytes 1179656 | tf_op jit(solution)/shard_map/ppermute | solution.py:27
  58.2 21.4 %collective-permute-start.6 = (bf16[464,512]{1,0:T(8,128)(2,1)}, bf16[464,512]{1,0:T(8,128)(2,1)}, u32[]{:S(2)}, u32[]{:S(2)}) collective-permute-start(bf16[464,512]{1,0:T(8,128)(2,1)} %collective-permute-done.5.refs_3_), channel_id=1, source_target_pairs={{0,7},{1,2},{2,1},{3,4},{4,3},{5,6},{6,5},{7,0},{8,15},{9,10},{10,... | collective-permute-start | bytes 1425416 | tf_op jit(solution)/shard_map/ppermute | solution.py:28
  63.1 12.5 %collective-permute-start.2 = (bf16[384,512]{1,0:T(8,128)(2,1)}, bf16[384,512]{1,0:T(8,128)(2,1)}, u32[]{:S(2)}, u32[]{:S(2)}) collective-permute-start(bf16[384,512]{1,0:T(8,128)(2,1)} %collective-permute-done.1.refs_11_), channel_id=1, source_target_pairs={{0,1},{1,0},{2,3},{3,2},{4,5},{5,4},{6,7},{7,6},{8,9},{9,8},{10,11... | collective-permute-start | bytes 1179656 | tf_op jit(solution)/shard_map/ppermute | solution.py:27
  66.8 23.8 %collective-permute-start.13 = (bf16[384,512]{1,0:T(8,128)(2,1)}, bf16[384,512]{1,0:T(8,128)(2,1)}, u32[]{:S(2)}, u32[]{:S(2)}) collective-permute-start(bf16[384,512]{1,0:T(8,128)(2,1)} %collective-permute-done.12.refs_10_), channel_id=1, source_target_pairs={{0,7},{1,2},{2,1},{3,4},{4,3},{5,6},{6,5},{7,0},{8,15},{9,10},{10,... | collective-permute-start | bytes 1179656 | tf_op jit(solution)/shard_map/ppermute | solution.py:28
  71.1 19.5 %collective-permute-start.10 = (bf16[464,512]{1,0:T(8,128)(2,1)}, bf16[464,512]{1,0:T(8,128)(2,1)}, u32[]{:S(2)}, u32[]{:S(2)}) collective-permute-start(bf16[464,512]{1,0:T(8,128)(2,1)} %collective-permute-done.9.refs_4_), channel_id=1, source_target_pairs={{0,1},{1,0},{2,3},{3,2},{4,5},{5,4},{6,7},{7,6},{8,9},{9,8},{10,11... | collective-permute-start | bytes 1425416 | tf_op jit(solution)/shard_map/ppermute | solution.py:27
  75.6 23.4 %collective-permute-start.3 = (bf16[384,512]{1,0:T(8,128)(2,1)}, bf16[384,512]{1,0:T(8,128)(2,1)}, u32[]{:S(2)}, u32[]{:S(2)}) collective-permute-start(bf16[384,512]{1,0:T(8,128)(2,1)} %collective-permute-done.2.refs_12_), channel_id=1, source_target_pairs={{0,7},{1,2},{2,1},{3,4},{4,3},{5,6},{6,5},{7,0},{8,15},{9,10},{10,... | collective-permute-start | bytes 1179656 | tf_op jit(solution)/shard_map/ppermute | solution.py:33
  79.6 16.7 %collective-permute-start.7 = (bf16[464,512]{1,0:T(8,128)(2,1)}, bf16[464,512]{1,0:T(8,128)(2,1)}, u32[]{:S(2)}, u32[]{:S(2)}) collective-permute-start(bf16[464,512]{1,0:T(8,128)(2,1)} %collective-permute-done.6.refs_6_), channel_id=1, source_target_pairs={{0,1},{1,0},{2,3},{3,2},{4,5},{5,4},{6,7},{7,6},{8,9},{9,8},{10,11... | collective-permute-start | bytes 1425416 | tf_op jit(solution)/shard_map/ppermute | solution.py:32
  90.6 1.0 copy-start.3
  100.6 26.8 %copy-start.5 = (s32[256,3]{0,1:T(4,128)S(1)}, s32[256,3]{0,1:T(4,128)}, u32[]{:S(2)}) copy-start(s32[256,3]{0,1:T(4,128)} %param.21) | copy-start | bytes 9220
  113.3 14.1 %all-to-all-start.3 = ((f32[8,1,3072]{2,1,0:T(1,128)}), f32[8,1,3072]{2,1,0:T(1,128)S(1)}, u32[]{:S(2)}, u32[]{:S(2)}) async-start(f32[8,1,3072]{2,1,0:T(1,128)} %shard_map.127), calls=%async_computation.3 | async-start | bytes 196608 | tf_op jit(solution)/shard_map/all_to_all | solution.py:385
